TPU v7x, 32 devices: a whole 2x2x4 slice. The times are simulated.
32 devices in a mesh: dp: 8 (over y, x, core), tensor: 4 (over z).
Axes of the slice: x: 2, y: 2, z: 4, core: 2. Of those that a mesh axis runs over, the one named last changes fastest.
Arguments:
- hidden_in: bfloat16 [8192, 2048], P(('dp', 'tensor')), may hold values from -6 to 6
- qkv_weight: bfloat16 [3, 2048, 2048], P(None, 'dp', 'tensor'), may hold values from -0.125 to 0.125
- head_bias: float32 [3, 2048], P(None, 'tensor'), may hold values from -3 to 3
- dense_weight: bfloat16 [2048, 2048], P('tensor', 'dp'), may hold values from -1 to 1
- dense_bias: float32 [2048], replicated, may hold values from -3 to 3
- fc1_weight: bfloat16 [2048, 8192], P('dp', 'tensor'), may hold values from -0.125 to 0.125
- fc1_bias: float32 [8192], P('tensor'), may hold values from -3 to 3
- fc2_weight: bfloat16 [8192, 2048], P('tensor', 'dp'), may hold values from -0.0625 to 0.0625
- fc2_bias: float32 [2048], replicated, may hold values from -3 to 3
- norm_gain: float32 [2048], replicated, may hold values from 0.5 to 1.5
- norm_bias: float32 [2048], replicated, may hold values from -2 to 2
- out_grad: bfloat16 [8192, 2048], P(('dp', 'tensor')), may hold values from -6 to 6
Outputs:
- hidden_out: bfloat16 [8192, 2048], P(('dp', 'tensor'))
- hidden_grad: bfloat16 [8192, 2048], P(('dp', 'tensor'))
- qkv_weight_grad: float32 [3, 2048, 2048], P(None, 'dp', 'tensor')
- head_bias_grad: float32 [3, 2048], P(None, 'tensor')
- dense_weight_grad: float32 [2048, 2048], P('tensor', 'dp')
- dense_bias_grad: float32 [2048], replicated
- fc1_weight_grad: float32 [2048, 8192], P('dp', 'tensor')
- fc1_bias_grad: float32 [8192], P('tensor')
- fc2_weight_grad: float32 [8192, 2048], P('tensor', 'dp')
- fc2_bias_grad: float32 [2048], replicated
- norm_gain_grad: float32 [2048], replicated
- norm_bias_grad: float32 [2048], replicated
All inputs are finite; a program needn't handle non-finite values.
Results may differ from a plain program's by a relative error of at most 0.0095.
Values may be sent and summed in bfloat16 or wider, within the bound.
A program may use at most 256 MiB of HBM per device.

v0:
```python
import math
import jax
import jax.numpy as jnp
from jax import lax
from jax.sharding import PartitionSpec as P

HD = 64
ROT = 32
SEQ_LEN = 1024


def dot_right(left, right):
    return lax.dot_general(
        left, right, (((1,), (1,)), ((), ())), preferred_element_type=jnp.float32
    )


def dot_left(left, right):
    return lax.dot_general(
        left, right, (((0,), (0,)), ((), ())), preferred_element_type=jnp.float32
    )


def gelu_tanh(values):
    return (
        0.5
        * values
        * (1.0 + jnp.tanh(0.7978845608028654 * (values + 0.044715 * values * values * values)))
    )


def rotate(values, sign):
    length = values.shape[0]
    half = ROT // 2
    freqs = 1.0 / 10000.0 ** (jnp.arange(half, dtype=jnp.float32) * 2.0 / ROT)
    positions = (jnp.arange(length) % SEQ_LEN).astype(jnp.float32)
    angles = positions[:, None] * freqs[None, :]
    cosine = jnp.cos(angles)[:, None, :]
    sine = sign * jnp.sin(angles)[:, None, :]
    first = values[..., :half]
    second = values[..., half:ROT]
    return jnp.concatenate(
        [first * cosine - second * sine, second * cosine + first * sine, values[..., ROT:]], axis=-1
    )


def masked_scores(queries, keys, start, finish, scale):
    scores = (
        jnp.einsum(
            "sqhd,skhd->shqk",
            queries[:, start:finish],
            keys[:, :finish],
            preferred_element_type=jnp.float32,
        )
        * scale
    )
    causal = jnp.arange(finish)[None, :] <= (jnp.arange(finish - start) + start)[:, None]
    return jnp.where(causal, scores, -1e30)


def attend(queries, keys, values):
    length = queries.shape[1]
    block = min(512, length)
    scale = 1.0 / math.sqrt(queries.shape[3])
    outputs = []
    logsums = []
    for block_index in range(length // block):
        start = block_index * block
        finish = start + block
        scores = masked_scores(queries, keys, start, finish, scale)
        largest = jnp.max(scores, axis=-1, keepdims=True)
        expos = jnp.exp(scores - largest)
        summed = jnp.sum(expos, axis=-1, keepdims=True)
        probs = (expos / summed).astype(jnp.bfloat16)
        outputs.append(
            jnp.einsum(
                "shqk,skhd->sqhd", probs, values[:, :finish], preferred_element_type=jnp.float32
            )
        )
        logsums.append((largest + jnp.log(summed))[..., 0])
    return (jnp.concatenate(outputs, axis=1), jnp.concatenate(logsums, axis=2))


def attend_back(queries, keys, values, grads_out, logsum):
    length = queries.shape[1]
    block = min(512, length)
    scale = 1.0 / math.sqrt(queries.shape[3])
    query_grads = []
    key_grad = jnp.zeros(keys.shape, jnp.float32)
    value_grad = jnp.zeros(values.shape, jnp.float32)
    for block_index in range(length // block):
        start = block_index * block
        finish = start + block
        scores = masked_scores(queries, keys, start, finish, scale)
        probs = jnp.exp(scores - logsum[:, :, start:finish, None])
        products = jnp.einsum(
            "sqhd,skhd->shqk",
            grads_out[:, start:finish],
            values[:, :finish],
            preferred_element_type=jnp.float32,
        )
        inner = jnp.sum(probs * products, axis=-1, keepdims=True)
        score_grad = (probs * (products - inner)).astype(jnp.bfloat16)
        query_grads.append(
            jnp.einsum(
                "shqk,skhd->sqhd", score_grad, keys[:, :finish], preferred_element_type=jnp.float32
            )
            * scale
        )
        key_grad = key_grad.at[:, :finish].add(
            jnp.einsum(
                "shqk,sqhd->skhd",
                score_grad,
                queries[:, start:finish],
                preferred_element_type=jnp.float32,
            )
            * scale
        )
        value_grad = value_grad.at[:, :finish].add(
            jnp.einsum(
                "shqk,sqhd->skhd",
                probs.astype(jnp.bfloat16),
                grads_out[:, start:finish],
                preferred_element_type=jnp.float32,
            )
        )
    return (jnp.concatenate(query_grads, axis=1), key_grad, value_grad)


def per_device(
    hidden_in,
    qkv_weight,
    head_bias,
    dense_weight,
    dense_bias,
    fc1_weight,
    fc1_bias,
    fc2_weight,
    fc2_bias,
    norm_gain,
    norm_bias,
    out_grad,
):
    qkv_full, dense_full, fc1_full, fc2_full = (
        lax.all_gather(qkv_weight, "dp", axis=1, tiled=True),
        lax.all_gather(dense_weight, "dp", axis=1, tiled=True),
        lax.all_gather(fc1_weight, "dp", axis=0, tiled=True),
        lax.all_gather(fc2_weight, "dp", axis=1, tiled=True),
    )
    inputs = hidden_in.astype(jnp.float32)
    centred = inputs - jnp.mean(inputs, axis=-1, keepdims=True)
    inverse_std = lax.rsqrt(jnp.mean(centred * centred, axis=-1, keepdims=True) + 1e-05)
    standard = centred * inverse_std
    normed = (standard * norm_gain + norm_bias).astype(jnp.bfloat16)
    normed_all = lax.all_gather(normed, "tensor", axis=0, tiled=True)
    rows = normed_all.shape[0]
    count = rows // SEQ_LEN
    width_local = qkv_full.shape[2]
    heads_local = width_local // HD

    def split_heads(values):
        return values.reshape(count, SEQ_LEN, heads_local, HD)

    projected = (
        jnp.einsum("td,cde->cte", normed_all, qkv_full, preferred_element_type=jnp.float32)
        + head_bias[:, None, :]
    )
    queries = rotate(projected[0].reshape(rows, heads_local, HD), 1.0).astype(jnp.bfloat16)
    keys = rotate(projected[1].reshape(rows, heads_local, HD), 1.0).astype(jnp.bfloat16)
    values = projected[2].astype(jnp.bfloat16).reshape(rows, heads_local, HD)
    mixed, logsum = attend(split_heads(queries), split_heads(keys), split_heads(values))
    mixed = mixed.reshape(rows, width_local).astype(jnp.bfloat16)
    hidden = jnp.dot(normed_all, fc1_full, preferred_element_type=jnp.float32) + fc1_bias
    active = gelu_tanh(hidden).astype(jnp.bfloat16)
    partial_value = jnp.dot(mixed, dense_full, preferred_element_type=jnp.float32) + jnp.dot(
        active, fc2_full, preferred_element_type=jnp.float32
    )
    summed = lax.psum_scatter(partial_value, "tensor", scatter_dimension=0, tiled=True)
    hidden_out = (inputs + summed + dense_bias + fc2_bias).astype(jnp.bfloat16)
    qkv_back, dense_back, fc1_back, fc2_back = (qkv_full, dense_full, fc1_full, fc2_full)
    grad_all = lax.all_gather(out_grad, "tensor", axis=0, tiled=True)
    feed_grad = dot_right(grad_all, fc2_back)
    unused, gelu_pull = jax.vjp(gelu_tanh, hidden)
    hidden_back = gelu_pull(feed_grad)[0].astype(jnp.bfloat16)
    fc2_grad = dot_left(active, grad_all)
    fc1_grad = dot_left(normed_all, hidden_back)
    fc1_bias_part = jnp.sum(hidden_back.astype(jnp.float32), axis=0)
    normed_back = dot_right(hidden_back, fc1_back)
    mixed_back = dot_right(grad_all, dense_back).astype(jnp.bfloat16)
    dense_grad = dot_left(mixed, grad_all)
    query_back, key_back, value_back = attend_back(
        split_heads(queries),
        split_heads(keys),
        split_heads(values),
        split_heads(mixed_back),
        logsum,
    )
    query_back = rotate(query_back.reshape(rows, heads_local, HD), -1.0).reshape(rows, width_local)
    key_back = rotate(key_back.reshape(rows, heads_local, HD), -1.0).reshape(rows, width_local)
    proj_back = jnp.stack([query_back, key_back, value_back.reshape(rows, width_local)]).astype(
        jnp.bfloat16
    )
    qkv_grad = jnp.einsum("td,cte->cde", normed_all, proj_back, preferred_element_type=jnp.float32)
    head_bias_part = jnp.sum(proj_back.astype(jnp.float32), axis=1)
    normed_back = normed_back + jnp.einsum(
        "cte,cde->td", proj_back, qkv_back, preferred_element_type=jnp.float32
    )
    own_back = lax.psum_scatter(normed_back, "tensor", scatter_dimension=0, tiled=True)
    scaled = own_back * norm_gain
    hidden_grad = out_grad.astype(jnp.float32) + inverse_std * (
        scaled
        - jnp.mean(scaled, axis=-1, keepdims=True)
        - standard * jnp.mean(scaled * standard, axis=-1, keepdims=True)
    )
    gain_part = jnp.sum(own_back * standard, axis=0)
    shift_part = jnp.sum(own_back, axis=0)
    output_part = jnp.sum(out_grad.astype(jnp.float32), axis=0)
    gain_grad, shift_grad, output_bias_grad = lax.psum(
        (gain_part, shift_part, output_part), ("dp", "tensor")
    )
    head_bias_grad, fc1_bias_grad = lax.psum((head_bias_part, fc1_bias_part), "dp")
    qkv_grad, dense_grad, fc1_grad, fc2_grad = (
        lax.psum_scatter(qkv_grad, "dp", scatter_dimension=1, tiled=True),
        lax.psum_scatter(dense_grad, "dp", scatter_dimension=1, tiled=True),
        lax.psum_scatter(fc1_grad, "dp", scatter_dimension=0, tiled=True),
        lax.psum_scatter(fc2_grad, "dp", scatter_dimension=1, tiled=True),
    )
    return (
        hidden_out,
        hidden_grad.astype(jnp.bfloat16),
        qkv_grad,
        head_bias_grad,
        dense_grad,
        output_bias_grad,
        fc1_grad,
        fc1_bias_grad,
        fc2_grad,
        output_bias_grad,
        gain_grad,
        shift_grad,
    )


def solution(mesh):
    placed = (
        P(("dp", "tensor"), None),
        P(None, "dp", "tensor"),
        P(None, "tensor"),
        P("tensor", "dp"),
        P(),
        P("dp", "tensor"),
        P("tensor"),
        P("tensor", "dp"),
        P(),
        P(),
        P(),
        P(("dp", "tensor"), None),
    )
    return jax.shard_map(
        per_device,
        mesh=mesh,
        in_specs=placed,
        out_specs=(
            P(("dp", "tensor"), None),
            P(("dp", "tensor"), None),
            P(None, "dp", "tensor"),
            P(None, "tensor"),
            P("tensor", "dp"),
            P(),
            P("dp", "tensor"),
            P("tensor"),
            P("tensor", "dp"),
            P(),
            P(),
            P(),
        ),
        check_vma=False,
    )
```

profile of v0, /device:TPU:0, one launch (start us, length us, event | category | flops | bytes accessed | tf_op | source)
XLA Modules:
  0.0 1059.4 jit_solution(7889824522170710664)
XLA Ops:
  19.7 21.1 %all-gather.11.cloned.1.call-done = bf16[512,2048]{1,0:T(8,128)(2,1)} async-done(((bf16[512,256]{1,0:T(8,128)(2,1)}), bf16[512,2048]{1,0:T(8,128)(2,1)}) %all-gather.11.cloned.1.call-update) | async-done | bytes 2097168 | tf_op jit(solution)/shard_map/all_gather | solution.py:146
  40.7 82.3 %all-gather.17.cloned.1.call-done = bf16[1024,2048]{1,0:T(8,128)(2,1)} async-done(((bf16[256,2048]{1,0:T(8,128)(2,1)}), bf16[1024,2048]{1,0:T(8,128)(2,1)}) %all-gather.17.cloned.1.call-update) | async-done | bytes 4194320 | tf_op jit(solution)/shard_map/all_gather | solution.py:181
  123.1 6.2 convolution_convert_fusion
  129.3 75.2 %all-gather.7.cloned.1.call-done = bf16[1024,2048]{1,0:T(8,128)(2,1)} async-done(((bf16[256,2048]{1,0:T(8,128)(2,1)}), bf16[1024,2048]{1,0:T(8,128)(2,1)}) %all-gather.7.cloned.1.call-update) | async-done | bytes 4194320 | tf_op jit(solution)/shard_map/all_gather | solution.py:155
  204.5 47.4 %all-gather.9.cloned.1.call-done = bf16[3,2048,512]{1,2,0:T(8,128)(2,1)} async-done(((bf16[3,256,512]{1,2,0:T(8,128)(2,1)}), bf16[3,2048,512]{1,2,0:T(8,128)(2,1)}) %all-gather.9.cloned.1.call-update) | async-done | bytes 6291472 | tf_op jit(solution)/shard_map/all_gather | solution.py:145
  251.9 10.6 %add_bitcast_fusion = f32[3,1024,512]{1,2,0:T(8,128)S(1)} fusion(f32[3,512]{1,0:T(4,128)S(1)} %copy-done.40, bf16[3,2048,512]{1,2,0:T(8,128)(2,1)} %all-gather.9.cloned.1.call-done, bf16[1024,2048]{1,0:T(8,128)(2,1)} %all-gather.7.cloned.1.call-done), kind=kOutput, calls=%fused_computation.33 | convolution fusion | flops 6444023808 | bytes 16783360 | tf_op jit(solution)/shard_map/td,cde->cte/dot_general | solution.py:165
  276.6 5.5 copy-done.2
  290.5 7.6 multiply_reduce_fusion.1
  298.0 7.4 multiply_convert_fusion.1
  309.4 9.9 multiply_reduce_fusion
  319.3 10.4 multiply_convert_fusion
  329.7 6.3 fusion.49
  347.1 12.4 %convolution_bitcast_fusion = f32[3,2048,512]{1,2,0:T(8,128)} fusion(bf16[1024,2048]{1,0:T(8,128)(2,1)} %all-gather.7.cloned.1.call-done, bf16[1,1024,512]{2,1,0:T(8,128)(2,1)S(1)} %copy-done.7, bf16[1,1024,512]{2,1,0:T(8,128)(2,1)} %copy.30, bf16[1,1024,512]{2,1,0:T(8,128)(2,1)} %copy.29), kind=kOutput, calls=%fused_computation.34 | convolution fusion | flops 6445596672 | bytes 19922944 | tf_op jit(solution)/shard_map/td,cte->cde/dot_general | solution.py:203
  359.6 14.6 %fusion.74 = f32[1024,2048]{1,0:T(8,128)} fusion(bf16[1024,2048]{1,0:T(8,128)(2,1)} %all-gather.7.cloned.1.call-done, bf16[2048,2048]{1,0:T(8,128)(2,1)} %all-gather.13.cloned.1.call-done), kind=kOutput, calls=%fused_computation.141 | convolution fusion | flops 8589934592 | bytes 20971520 | tf_op jit(solution)/shard_map/dot_general | solution.py:173
  374.2 22.7 %convert_reduce_fusion = (f32[2048]{0:T(1024)}, bf16[1024,2048]{1,0:T(8,128)(2,1)S(1)}) fusion(f32[1024,2048]{1,0:T(8,128)} %fusion.74, f32[2048]{0:T(1024)S(1)} %copy-done.41, bf16[1024,2048]{1,0:T(8,128)(2,1)} %all-gather.17.cloned.1.call-done, bf16[2048,2048]{1,0:T(8,128)(2,1)} %all-gather.15.cloned.1.call-done), kind=kOutput, calls=%fused_computation.20 | convolution fusion | flops 8646555648 | bytes 25182208 | tf_op jit(solution)/shard_map/dot_general | solution.py:13
  396.8 11.7 %fusion.75 = f32[1024,2048]{1,0:T(8,128)} fusion(bf16[1024,2048]{1,0:T(8,128)(2,1)S(1)} %get-tuple-element.98, bf16[2048,2048]{1,0:T(8,128)(2,1)S(1)} %copy-done.39), kind=kOutput, calls=%fused_computation.142 | convolution fusion | flops 8589934592 | bytes 20971520 | tf_op jit(solution)/shard_map/dot_general | solution.py:13
  408.5 13.2 %bitcast_add_fusion = f32[1024,2048]{1,0:T(8,128)} fusion(f32[1024,2048]{1,0:T(8,128)} %fusion.75, bf16[3,2048,512]{1,2,0:T(8,128)(2,1)} %all-gather.9.cloned.1.call-done, bf16[1,1024,512]{2,1,0:T(8,128)(2,1)S(1)} %copy-done.7, bf16[1,1024,512]{2,1,0:T(8,128)(2,1)S(1)} %copy-done.9, bf16[1,1024,512]{2,1,0:T(8,128)(2,1)S(1)} %copy-done.8), kind=kOutput, calls=%fused_computation.19 | convolution fusion | flops 6447693824 | bytes 26214400 | tf_op jit(solution)/shard_map/cte,cde->td/dot_general | solution.py:205
  422.4 5.0 fusion.53
  427.4 8.0 fusion.52
  435.6 12.2 %fusion.69 = f32[1024,2048]{1,0:T(8,128)S(1)} fusion(bf16[2048,2048]{1,0:T(8,128)(2,1)S(1)} %bitcast.159, f32[1024,2048]{1,0:T(8,128)} %fusion.74, f32[2048]{0:T(1024)S(1)} %copy-done.41), kind=kOutput, calls=%fused_computation.136 | convolution fusion | flops 8610906112 | bytes 25174016 | tf_op jit(solution)/shard_map/dot_general | solution.py:175
  447.8 5.7 convolution_add_fusion
  453.6 6.5 fusion.76
  460.2 17.5 %fusion.68 = f32[2048,2048]{1,0:T(8,128)} fusion(bf16[1024,2048]{1,0:T(8,128)(2,1)} %all-gather.17.cloned.1.call-done, f32[1024,2048]{1,0:T(8,128)} %fusion.74, f32[2048]{0:T(1024)S(1)} %copy-done.41), kind=kOutput, calls=%fused_computation.135 | convolution fusion | flops 8610906112 | bytes 29368320 | tf_op jit(solution)/shard_map/dot_general | solution.py:19
  477.7 15.5 %fusion.77 = f32[2048,2048]{1,0:T(8,128)} fusion(bf16[1024,2048]{1,0:T(8,128)(2,1)} %all-gather.7.cloned.1.call-done, bf16[1024,2048]{1,0:T(8,128)(2,1)} %copy-done.42), kind=kOutput, calls=%fused_computation.144 | convolution fusion | flops 8589934592 | bytes 25165824 | tf_op jit(solution)/shard_map/dot_general | solution.py:19
  495.4 24.6 %all-reduce.3 = (f32[3,512]{1,0:T(4,128)}, f32[2048]{0:T(1024)}) all-reduce(f32[3,512]{1,0:T(4,128)S(1)} %convert_reduce_fusion.1, f32[2048]{0:T(1024)S(1)} %copy-done.35), channel_id=1, replica_groups=mesh['dp'=8,'tensor'=4] {'dp'}, use_global_device_ids=true, to_apply=%region_14.15 | all-reduce | flops 3584 | bytes 28672 | tf_op jit(solution)/shard_map/psum | solution.py:221
  523.0 85.0 %reduce-scatter.9.cloned.1.call-done = f32[256,2048]{1,0:T(8,128)} async-done(((f32[1024,2048]{1,0:T(8,128)}), f32[256,2048]{1,0:T(8,128)}) %reduce-scatter.9.cloned.1.call-update) | async-done | bytes 2097168 | tf_op jit(solution)/shard_map/reduce_scatter | solution.py:208
  610.7 145.0 %reduce-scatter.7.cloned.1.call-done = f32[256,2048]{1,0:T(8,128)} async-done(((f32[1024,2048]{1,0:T(8,128)}), f32[256,2048]{1,0:T(8,128)}) %reduce-scatter.7.cloned.1.call-update) | async-done | bytes 2097168 | tf_op jit(solution)/shard_map/reduce_scatter | solution.py:178
  755.7 5.1 convert_reduce_fusion.3
  760.8 41.3 %all-reduce.2 = (f32[2048]{0:T(1024)S(1)}, f32[2048]{0:T(1024)}, f32[2048]{0:T(1024)}) all-reduce(f32[2048]{0:T(1024)S(1)} %get-tuple-element.109, f32[2048]{0:T(1024)S(1)} %get-tuple-element.88, f32[2048]{0:T(1024)S(1)} %get-tuple-element.91), channel_id=1, replica_groups=mesh['dp'=8,'tensor'=4] {'dp','tensor'}, use_global_device_ids=true, to_apply=%region_17.18 | all-reduce | flops 6144 | bytes 49152 | tf_op jit(solution)/shard_map/psum | solution.py:218
  802.1 9.2 reduce-scatter.13.cloned.1.call-done
  811.3 120.2 %reduce-scatter.17.cloned.1.call-done = f32[2048,256]{1,0:T(8,128)} async-done(((f32[2048,2048]{1,0:T(8,128)}), f32[2048,256]{1,0:T(8,128)}) %reduce-scatter.17.cloned.1.call-update) | async-done | bytes 2097168 | tf_op jit(solution)/shard_map/reduce_scatter | solution.py:226
  931.5 120.2 %reduce-scatter.15.cloned.1.call-done = f32[256,2048]{1,0:T(8,128)} async-done(((f32[2048,2048]{1,0:T(8,128)}), f32[256,2048]{1,0:T(8,128)}) %reduce-scatter.15.cloned.1.call-update) | async-done | bytes 2097168 | tf_op jit(solution)/shard_map/reduce_scatter | solution.py:225
  (176 shorter events, 58.9 us)
Async XLA Ops:
  7.2 33.5 %all-gather.11.cloned.1.call-start = ((), (), s32[]{:S(2)}) async-start(), calls=%async_computation.8 | async-start | bytes 2359296 | tf_op jit(solution)/shard_map/all_gather | solution.py:146
  7.9 115.1 %all-gather.17.cloned.1.call-start = ((), (), s32[]{:S(2)}) async-start(), calls=%async_computation.12 | async-start | bytes 5242880 | tf_op jit(solution)/shard_map/all_gather | solution.py:181
  8.7 195.8 %all-gather.7.cloned.1.call-start = ((), (), s32[]{:S(2)}) async-start(), calls=%async_computation.6 | async-start | bytes 5242880 | tf_op jit(solution)/shard_map/all_gather | solution.py:155
  15.1 236.8 %all-gather.9.cloned.1.call-start = ((), (), s32[]{:S(2)}) async-start(), calls=%async_computation.7 | async-start | bytes 7077888 | tf_op jit(solution)/shard_map/all_gather | solution.py:145
  16.3 343.2 %all-gather.13.cloned.1.call-start = ((), (), s32[]{:S(2)}) async-start(), calls=%async_computation.9 | async-start | bytes 9437184 | tf_op jit(solution)/shard_map/all_gather | solution.py:147
  16.9 357.2 %all-gather.15.cloned.1.call-start = ((), (), s32[]{:S(2)}) async-start(), calls=%async_computation.10 | async-start | bytes 9437184 | tf_op jit(solution)/shard_map/all_gather | solution.py:148
  17.5 502.5 %reduce-scatter.11.cloned.1.call-start = ((), (), s32[]{:S(2)}) async-start(), calls=%async_computation.14 | async-start | bytes 14155776 | tf_op jit(solution)/shard_map/reduce_scatter | solution.py:223
  19.7 243.7 %copy-start.17 = (f32[1024,16]{0,1:T(8,128)}, f32[1024,16]{0,1:T(8,128)S(1)}, u32[]{:S(2)}) copy-start(f32[1024,16]{0,1:T(8,128)S(1)} %get-tuple-element.118) | copy-start | bytes 196612
  19.7 232.2 %copy-start.40 = (f32[3,512]{1,0:T(4,128)S(1)}, f32[3,512]{1,0:T(4,128)}, u32[]{:S(2)}) copy-start(f32[3,512]{1,0:T(4,128)} %param.26) | copy-start | bytes 18436
  269.6 20.8 %copy-start.21 = (f32[8,512]{1,0:T(8,128)}, f32[8,512]{1,0:T(8,128)S(1)}, u32[]{:S(2)}) copy-start(f32[8,512]{1,0:T(8,128)S(1)} %log_add_fusion.1) | copy-start | bytes 49156
  290.4 18.9 %slice-start = ((s8[16777216]{0:T(1024)(128)(4,1)}), s8[4194304]{0:T(1024)(128)(4,1)S(1)}, s32[]{:S(2)}) async-start(s8[16777216]{0:T(1024)(128)(4,1)} %bitcast.132), calls=%async_computation.18 | async-start | bytes 8388608
  290.4 19.0 %slice-start.1 = ((s8[16777216]{0:T(1024)(128)(4,1)}), s8[4194304]{0:T(1024)(128)(4,1)S(1)}, s32[]{:S(2)}) async-start(s8[16777216]{0:T(1024)(128)(4,1)} %bitcast.132), calls=%async_computation.19 | async-start | bytes 8388608
  359.5 14.7 %copy-start.41 = (f32[2048]{0:T(1024)S(1)}, f32[2048]{0:T(1024)}, u32[]{:S(2)}) copy-start(f32[2048]{0:T(1024)} %param.30) | copy-start | bytes 24580
  359.5 248.5 %reduce-scatter.9.cloned.1.call-start = ((), (), s32[]{:S(2)}) async-start(), calls=%async_computation.13 | async-start | bytes 10485760 | tf_op jit(solution)/shard_map/reduce_scatter | solution.py:208
  374.2 22.7 %copy-start.39 = (bf16[2048,2048]{1,0:T(8,128)(2,1)S(1)}, bf16[2048,2048]{1,0:T(8,128)(2,1)}, u32[]{:S(2)}) copy-start(bf16[2048,2048]{1,0:T(8,128)(2,1)} %all-gather.13.cloned.1.call-done) | copy-start | bytes 25165828
  396.8 11.7 %copy-start.42 = (bf16[1024,2048]{1,0:T(8,128)(2,1)}, bf16[1024,2048]{1,0:T(8,128)(2,1)S(1)}, u32[]{:S(2)}) copy-start(bf16[1024,2048]{1,0:T(8,128)(2,1)S(1)} %get-tuple-element.98) | copy-start | bytes 12582916
  396.8 11.7 %copy-start.8 = (bf16[1,1024,512]{2,1,0:T(8,128)(2,1)S(1)}, bf16[1,1024,512]{2,1,0:T(8,128)(2,1)}, u32[]{:S(2)}) copy-start(bf16[1,1024,512]{2,1,0:T(8,128)(2,1)} %copy.29) | copy-start | bytes 3145732
  396.8 11.7 %copy-start.9 = (bf16[1,1024,512]{2,1,0:T(8,128)(2,1)S(1)}, bf16[1,1024,512]{2,1,0:T(8,128)(2,1)}, u32[]{:S(2)}) copy-start(bf16[1,1024,512]{2,1,0:T(8,128)(2,1)} %copy.30) | copy-start | bytes 3145732
  421.7 333.9 %reduce-scatter.7.cloned.1.call-start = ((), (), s32[]{:S(2)}) async-start(), calls=%async_computation.11 | async-start | bytes 10485760 | tf_op jit(solution)/shard_map/reduce_scatter | solution.py:178
  422.4 13.2 %slice-start.6 = ((s8[8388608]{0:T(1024)(128)(4,1)}), s8[4194304]{0:T(1024)(128)(4,1)S(1)}, s32[]{:S(2)}) async-start(s8[8388608]{0:T(1024)(128)(4,1)} %bitcast.158), calls=%async_computation.24 | async-start | bytes 8388608
  435.6 12.2 %copy-start.12 = (bf16[512,2048]{1,0:T(8,128)(2,1)S(1)}, bf16[512,2048]{1,0:T(8,128)(2,1)}, u32[]{:S(2)}) copy-start(bf16[512,2048]{1,0:T(8,128)(2,1)} %all-gather.11.cloned.1.call-done) | copy-start | bytes 6291460
  453.5 357.8 %reduce-scatter.13.cloned.1.call-start = ((), (), s32[]{:S(2)}) async-start(), calls=%async_computation.15 | async-start | bytes 4718592 | tf_op jit(solution)/shard_map/reduce_scatter | solution.py:224
  460.1 471.4 %reduce-scatter.17.cloned.1.call-start = ((), (), s32[]{:S(2)}) async-start(), calls=%async_computation.17 | async-start | bytes 18874368 | tf_op jit(solution)/shard_map/reduce_scatter | solution.py:226
  477.7 574.0 %reduce-scatter.15.cloned.1.call-start = ((), (), s32[]{:S(2)}) async-start(), calls=%async_computation.16 | async-start | bytes 18874368 | tf_op jit(solution)/shard_map/reduce_scatter | solution.py:225
  493.2 114.8 %copy-start.5 = (bf16[256,2048]{1,0:T(8,128)(2,1)S(1)}, bf16[256,2048]{1,0:T(8,128)(2,1)}, u32[]{:S(2)}) copy-start(bf16[256,2048]{1,0:T(8,128)(2,1)} %param.24) | copy-start | bytes 3145732
  493.2 114.8 %copy-start.22 = (f32[2048]{0:T(1024)S(1)}, f32[2048]{0:T(1024)}, u32[]{:S(2)}) copy-start(f32[2048]{0:T(1024)} %param.33) | copy-start | bytes 24580
  493.2 114.8 %copy-start.32 = (f32[256]{0:T(256)S(1)}, f32[256]{0:T(256)}, u32[]{:S(2)}) copy-start(f32[256]{0:T(256)} %copy-done.31) | copy-start | bytes 3076
  493.3 114.8 %copy-start.34 = (f32[256]{0:T(256)S(1)}, f32[256]{0:T(256)}, u32[]{:S(2)}) copy-start(f32[256]{0:T(256)} %copy-done.33) | copy-start | bytes 3076
  493.3 262.4 %copy-start.37 = (f32[2048]{0:T(1024)S(1)}, f32[2048]{0:T(1024)}, u32[]{:S(2)}) copy-start(f32[2048]{0:T(1024)} %param.32) | copy-start | bytes 24580
  493.3 262.4 %copy-start.38 = (f32[2048]{0:T(1024)S(1)}, f32[2048]{0:T(1024)}, u32[]{:S(2)}) copy-start(f32[2048]{0:T(1024)} %param.28) | copy-start | bytes 24580
  495.4 260.3 %copy-start.11 = (bf16[256,2048]{1,0:T(8,128)(2,1)S(1)}, bf16[256,2048]{1,0:T(8,128)(2,1)}, u32[]{:S(2)}) copy-start(bf16[256,2048]{1,0:T(8,128)(2,1)} %param.35) | copy-start | bytes 3145732
  802.1 250.2 %copy-start.36 = (f32[2048]{0:T(1024)}, f32[2048]{0:T(1024)S(1)}, u32[]{:S(2)}) copy-start(f32[2048]{0:T(1024)S(1)} %get-tuple-element.150) | copy-start | bytes 24580
  (31 other events, 169.4 us)
Sparse Core Ops, SparseCore 0:
  9.9 30.8 all-gather.10
  42.3 80.7 all-gather.16
  125.2 79.2 all-gather.6
  206.8 45.0 all-gather.8
  253.6 54.2 all-gather.12
  309.6 55.8 all-gather.14
  369.0 91.9 reduce-scatter.10
  463.4 144.6 reduce-scatter.8
  610.4 145.1 reduce-scatter.6
  759.4 51.8 reduce-scatter.12
  815.4 116.0 reduce-scatter.16
  935.5 116.1 reduce-scatter.14
where the time goes:
time: 1060 us
  waiting for transfers between devices  708 us (67%)
  matrix products  200 us (19%)
  blocking collectives  65.9 us (6%)
  other arithmetic  42.9 us (4%)
  local copies, waits for them, and re-layouts  26.5 us (2%)
  between operations  15.2 us (1%)
    reduce_scatter x1, waiting for transfers between devices, per_device(): lax.psum_scatter(partial_value, 'tensor', scatter_dimension=0, tiled=True)  145 us
    reduce_scatter x1, waiting for transfers between devices, per_device(): lax.psum_scatter(fc1_grad, 'dp', scatter_dimension=0, tiled=True)  120 us
    reduce_scatter x1, waiting for transfers between devices, per_device(): lax.psum_scatter(fc2_grad, 'dp', scatter_dimension=1, tiled=True)  120 us
    reduce_scatter x1, waiting for transfers between devices, per_device(): lax.psum_scatter(normed_back, 'tensor', scatter_dimension=0, tiled=True)  85 us
    all_gather x1, waiting for transfers between devices, per_device(): grad_all = lax.all_gather(out_grad, 'tensor', axis=0, tiled=True)  82.3 us
    all_gather x1, waiting for transfers between devices, per_device(): normed_all = lax.all_gather(normed, 'tensor', axis=0, tiled=True)  75.2 us
    all_gather x1, waiting for transfers between devices, per_device(): lax.all_gather(qkv_weight, 'dp', axis=1, tiled=True)  47.4 us
    psum x1, blocking collectives, per_device(): lax.psum((gain_part, shift_part, output_part), ('dp', 'tensor'))  41.3 us
  transfers between devices with their start and end apart: 12, of which 9 were waited for; matrix products, arithmetic and copies ran while one was open for 24% of the time, Pallas kernels for 0%

commit v1 on v0

--- a/solution.py
+++ b/solution.py
@@ -178,7 +178,23 @@
     summed = lax.psum_scatter(partial_value, "tensor", scatter_dimension=0, tiled=True)
     hidden_out = (inputs + summed + dense_bias + fc2_bias).astype(jnp.bfloat16)
     qkv_back, dense_back, fc1_back, fc2_back = (qkv_full, dense_full, fc1_full, fc2_full)
-    grad_all = lax.all_gather(out_grad, "tensor", axis=0, tiled=True)
+    ways, here, step = (lax.axis_size("tensor"), lax.axis_index("tensor"), out_grad.shape[0])
+    lengths = [n * ways if d == 0 else n for d, n in enumerate(out_grad.shape)]
+    full = lax.dynamic_update_slice_in_dim(
+        jnp.zeros(lengths, out_grad.dtype), out_grad, here * step, axis=0
+    )
+    going_up = going_down = out_grad
+    for far in range(1, ways // 2 + 1):
+        going_up = lax.ppermute(going_up, "tensor", [(d, (d + 1) % ways) for d in range(ways)])
+        full = lax.dynamic_update_slice_in_dim(full, going_up, (here - far) % ways * step, axis=0)
+        if 2 * far < ways:
+            going_down = lax.ppermute(
+                going_down, "tensor", [(d, (d - 1) % ways) for d in range(ways)]
+            )
+            full = lax.dynamic_update_slice_in_dim(
+                full, going_down, (here + far) % ways * step, axis=0
+            )
+    grad_all = full
     feed_grad = dot_right(grad_all, fc2_back)
     unused, gelu_pull = jax.vjp(gelu_tanh, hidden)
     hidden_back = gelu_pull(feed_grad)[0].astype(jnp.bfloat16)

time: 1060 us -> 1020 us (0.962)
  waiting for transfers between devices: 708 us -> 649 us
    ppermute x0 -> x3, waiting for transfers between devices: none -> 95 us  [the longest x1 55.5 us: per_device(): lax.ppermute(going_down, 'tensor', [(d, (d - 1) % ways) for d in range(wa...]
    all_gather x1 -> x0, waiting for transfers between devices: 82.3 us -> none  [per_device(): grad_all = lax.all_gather(out_grad, 'tensor', axis=0, tiled=True)]
    all_gather x1, waiting for transfers between devices: 75.2 us -> 24.9 us  [per_device(): normed_all = lax.all_gather(normed, 'tensor', axis=0, tiled=True)]
    all_gather x1, waiting for transfers between devices: 21.1 us -> 0.01 us  [per_device(): lax.all_gather(dense_weight, 'dp', axis=1, tiled=True)]
  transfers between devices with their start and end apart: 12 -> 14, of which waited for: 9 -> 10; matrix products, arithmetic and copies ran while one was open for 24% -> 26% of each run, Pallas kernels for 0% -> 0%
where the time goes in v1:
time: 1020 us; the launch traced here: 1010 us
  waiting for transfers between devices  649 us (64%)
  matrix products  200 us (20%)
  blocking collectives  65.6 us (6%)
  other arithmetic  43.8 us (4%)
  local copies, waits for them, and re-layouts  34.6 us (3%)
  between operations  14.9 us (1%)
    reduce_scatter x1, waiting for transfers between devices, per_device(): lax.psum_scatter(partial_value, 'tensor', scatter_dimension=0, tiled=True)  145 us
    reduce_scatter x1, waiting for transfers between devices, per_device(): lax.psum_scatter(fc1_grad, 'dp', scatter_dimension=0, tiled=True)  120 us
    reduce_scatter x1, waiting for transfers between devices, per_device(): lax.psum_scatter(fc2_grad, 'dp', scatter_dimension=1, tiled=True)  120 us
    reduce_scatter x1, waiting for transfers between devices, per_device(): lax.psum_scatter(normed_back, 'tensor', scatter_dimension=0, tiled=True)  84.8 us
    ppermute x1, waiting for transfers between devices, per_device(): lax.ppermute(going_down, 'tensor', [(d, (d - 1) % ways) for d in range(wa...  55.5 us
    all_gather x1, waiting for transfers between devices, per_device(): lax.all_gather(qkv_weight, 'dp', axis=1, tiled=True)  48.2 us
    psum x1, blocking collectives, per_device(): lax.psum((gain_part, shift_part, output_part), ('dp', 'tensor'))  41.3 us
    dot_general x3, matrix products, dot_right(): lax.dot_general(left, right, (((1,), (1,)), ((), ())), preferred_element_...  40.7 us
  transfers between devices with their start and end apart: 14, of which 10 were waited for; matrix products, arithmetic and copies ran while one was open for 26% of the time, Pallas kernels for 0%

profile of v1, /device:TPU:0, one launch (start us, length us, event | category | flops | bytes accessed | tf_op | source)
XLA Modules:
  0.0 1014.0 jit_solution(15267071119040956395)
XLA Ops:
  24.5 22.1 %collective-permute-done = bf16[256,2048]{1,0:T(8,128)(2,1)S(1)} collective-permute-done((bf16[256,2048]{1,0:T(8,128)(2,1)S(1)}, bf16[256,2048]{1,0:T(8,128)(2,1)S(1)}, u32[]{:S(2)}, u32[]{:S(2)}) %collective-permute-start) | collective-permute-done | bytes 1048608 | tf_op jit(solution)/shard_map/ppermute | solution.py:188
  52.4 55.5 %collective-permute-done.1 = bf16[256,2048]{1,0:T(8,128)(2,1)S(1)} collective-permute-done((bf16[256,2048]{1,0:T(8,128)(2,1)S(1)}, bf16[256,2048]{1,0:T(8,128)(2,1)S(1)}, u32[]{:S(2)}, u32[]{:S(2)}) %collective-permute-start.1) | collective-permute-done | bytes 1048608 | tf_op jit(solution)/shard_map/ppermute | solution.py:191
  108.9 17.5 %collective-permute-done.2 = bf16[256,2048]{1,0:T(8,128)(2,1)S(1)} collective-permute-done((bf16[256,2048]{1,0:T(8,128)(2,1)S(1)}, bf16[256,2048]{1,0:T(8,128)(2,1)S(1)}, u32[]{:S(2)}, u32[]{:S(2)}) %collective-permute-start.2) | collective-permute-done | bytes 1048608 | tf_op jit(solution)/shard_map/ppermute | solution.py:188
  127.4 6.2 convolution_convert_fusion
  133.7 24.9 %all-gather.6.cloned.1.call-done = bf16[1024,2048]{1,0:T(8,128)(2,1)} async-done(((bf16[256,2048]{1,0:T(8,128)(2,1)}), bf16[1024,2048]{1,0:T(8,128)(2,1)}) %all-gather.6.cloned.1.call-update) | async-done | bytes 4194320 | tf_op jit(solution)/shard_map/all_gather | solution.py:155
  158.6 48.2 %all-gather.8.cloned.1.call-done = bf16[3,2048,512]{1,2,0:T(8,128)(2,1)} async-done(((bf16[3,256,512]{1,2,0:T(8,128)(2,1)}), bf16[3,2048,512]{1,2,0:T(8,128)(2,1)}) %all-gather.8.cloned.1.call-update) | async-done | bytes 6291472 | tf_op jit(solution)/shard_map/all_gather | solution.py:145
  206.8 10.6 %add_bitcast_fusion = f32[3,1024,512]{1,2,0:T(8,128)S(1)} fusion(f32[3,512]{1,0:T(4,128)S(1)} %copy-done.42, bf16[3,2048,512]{1,2,0:T(8,128)(2,1)} %all-gather.8.cloned.1.call-done, bf16[1024,2048]{1,0:T(8,128)(2,1)} %all-gather.6.cloned.1.call-done), kind=kOutput, calls=%fused_computation.33 | convolution fusion | flops 6444023808 | bytes 16783360 | tf_op jit(solution)/shard_map/td,cde->cte/dot_general | solution.py:165
  231.7 5.6 copy-done.2
  245.5 7.6 multiply_reduce_fusion.1
  253.1 7.4 multiply_convert_fusion.1
  264.5 9.9 multiply_reduce_fusion
  274.3 10.3 %multiply_convert_fusion = bf16[8,512,1024]{2,1,0:T(8,128)(2,1)} fusion(f32[8,512,1024]{2,1,0:T(8,128)} %get-tuple-element.126, f32[8,512,1024]{2,1,0:T(8,128)S(1)} %bitcast.133, f32[8,512]{1,0:T(8,128)} %get-tuple-element.125, f32[8,512]{1,0:T(8,128)S(1)} %log_add_fusion), kind=kLoop, calls=%fused_computation | loop fusion | flops 16777216 | bytes 41975808 | tf_op jit(solution)/shard_map/convert_element_type | solution.py:103
  284.7 6.4 fusion.49
  302.3 12.4 %convolution_bitcast_fusion = f32[3,2048,512]{1,2,0:T(8,128)} fusion(bf16[1024,2048]{1,0:T(8,128)(2,1)} %all-gather.6.cloned.1.call-done, bf16[1,1024,512]{2,1,0:T(8,128)(2,1)S(1)} %copy-done.7, bf16[1,1024,512]{2,1,0:T(8,128)(2,1)} %copy.30, bf16[1,1024,512]{2,1,0:T(8,128)(2,1)} %copy.29), kind=kOutput, calls=%fused_computation.34 | convolution fusion | flops 6445596672 | bytes 19922944 | tf_op jit(solution)/shard_map/td,cte->cde/dot_general | solution.py:219
  314.8 14.7 %fusion.74 = f32[1024,2048]{1,0:T(8,128)} fusion(bf16[1024,2048]{1,0:T(8,128)(2,1)} %all-gather.6.cloned.1.call-done, bf16[2048,2048]{1,0:T(8,128)(2,1)} %all-gather.12.cloned.1.call-done), kind=kOutput, calls=%fused_computation.145 | convolution fusion | flops 8589934592 | bytes 20971520 | tf_op jit(solution)/shard_map/dot_general | solution.py:173
  329.4 23.0 %convert_reduce_fusion = (f32[2048]{0:T(1024)}, bf16[1024,2048]{1,0:T(8,128)(2,1)S(1)}) fusion(f32[1024,2048]{1,0:T(8,128)} %fusion.74, f32[2048]{0:T(1024)S(1)} %copy-done.43, bf16[1024,2048]{1,0:T(8,128)(2,1)} %constant_dynamic-update-slice_fusion, bf16[2048,2048]{1,0:T(8,128)(2,1)} %all-gather.14.cloned.1.call-done), kind=kOutput, calls=%fused_computation.20 | convolution fusion | flops 8646555648 | bytes 25182208 | tf_op jit(solution)/shard_map/dot_general | solution.py:13
  352.4 11.5 %fusion.75 = f32[1024,2048]{1,0:T(8,128)} fusion(bf16[1024,2048]{1,0:T(8,128)(2,1)S(1)} %get-tuple-element.98, bf16[2048,2048]{1,0:T(8,128)(2,1)S(1)} %copy-done.41), kind=kOutput, calls=%fused_computation.146 | convolution fusion | flops 8589934592 | bytes 20971520 | tf_op jit(solution)/shard_map/dot_general | solution.py:13
  364.0 13.1 %bitcast_add_fusion = f32[1024,2048]{1,0:T(8,128)} fusion(f32[1024,2048]{1,0:T(8,128)} %fusion.75, bf16[3,2048,512]{1,2,0:T(8,128)(2,1)} %all-gather.8.cloned.1.call-done, bf16[1,1024,512]{2,1,0:T(8,128)(2,1)S(1)} %copy-done.7, bf16[1,1024,512]{2,1,0:T(8,128)(2,1)S(1)} %copy-done.9, bf16[1,1024,512]{2,1,0:T(8,128)(2,1)S(1)} %copy-done.8), kind=kOutput, calls=%fused_computation.19 | convolution fusion | flops 6447693824 | bytes 26214400 | tf_op jit(solution)/shard_map/cte,cde->td/dot_general | solution.py:221
  382.8 8.0 fusion.52
  391.0 12.2 %fusion.69 = f32[1024,2048]{1,0:T(8,128)S(1)} fusion(bf16[2048,2048]{1,0:T(8,128)(2,1)S(1)} %bitcast.159, f32[1024,2048]{1,0:T(8,128)} %fusion.74, f32[2048]{0:T(1024)S(1)} %copy-done.43), kind=kOutput, calls=%fused_computation.140 | convolution fusion | flops 8610906112 | bytes 25174016 | tf_op jit(solution)/shard_map/dot_general | solution.py:175
  403.2 5.7 convolution_add_fusion
  409.0 6.5 fusion.76
  415.5 17.4 %fusion.68 = f32[2048,2048]{1,0:T(8,128)} fusion(bf16[1024,2048]{1,0:T(8,128)(2,1)} %constant_dynamic-update-slice_fusion, f32[1024,2048]{1,0:T(8,128)} %fusion.74, f32[2048]{0:T(1024)S(1)} %copy-done.43), kind=kOutput, calls=%fused_computation.139 | convolution fusion | flops 8610906112 | bytes 29368320 | tf_op jit(solution)/shard_map/dot_general | solution.py:19
  433.1 15.4 %fusion.77 = f32[2048,2048]{1,0:T(8,128)} fusion(bf16[1024,2048]{1,0:T(8,128)(2,1)} %all-gather.6.cloned.1.call-done, bf16[1024,2048]{1,0:T(8,128)(2,1)} %copy-done.44), kind=kOutput, calls=%fused_computation.148 | convolution fusion | flops 8589934592 | bytes 25165824 | tf_op jit(solution)/shard_map/dot_general | solution.py:19
  450.6 24.3 %all-reduce.3 = (f32[3,512]{1,0:T(4,128)}, f32[2048]{0:T(1024)}) all-reduce(f32[3,512]{1,0:T(4,128)S(1)} %convert_reduce_fusion.1, f32[2048]{0:T(1024)S(1)} %copy-done.37), channel_id=1, replica_groups=mesh['dp'=8,'tensor'=4] {'dp'}, use_global_device_ids=true, to_apply=%region_14.15 | all-reduce | flops 3584 | bytes 28672 | tf_op jit(solution)/shard_map/psum | solution.py:237
  478.0 84.8 %reduce-scatter.9.cloned.1.call-done = f32[256,2048]{1,0:T(8,128)} async-done(((f32[1024,2048]{1,0:T(8,128)}), f32[256,2048]{1,0:T(8,128)}) %reduce-scatter.9.cloned.1.call-update) | async-done | bytes 2097168 | tf_op jit(solution)/shard_map/reduce_scatter | solution.py:224
  565.4 145.0 %reduce-scatter.7.cloned.1.call-done = f32[256,2048]{1,0:T(8,128)} async-done(((f32[1024,2048]{1,0:T(8,128)}), f32[256,2048]{1,0:T(8,128)}) %reduce-scatter.7.cloned.1.call-update) | async-done | bytes 2097168 | tf_op jit(solution)/shard_map/reduce_scatter | solution.py:178
  710.4 5.1 convert_reduce_fusion.3
  715.5 41.3 %all-reduce.2 = (f32[2048]{0:T(1024)S(1)}, f32[2048]{0:T(1024)}, f32[2048]{0:T(1024)}) all-reduce(f32[2048]{0:T(1024)S(1)} %get-tuple-element.109, f32[2048]{0:T(1024)S(1)} %get-tuple-element.88, f32[2048]{0:T(1024)S(1)} %get-tuple-element.91), channel_id=1, replica_groups=mesh['dp'=8,'tensor'=4] {'dp','tensor'}, use_global_device_ids=true, to_apply=%region_17.18 | all-reduce | flops 6144 | bytes 49152 | tf_op jit(solution)/shard_map/psum | solution.py:234
  756.9 9.4 reduce-scatter.13.cloned.1.call-done
  766.3 120.0 %reduce-scatter.17.cloned.1.call-done = f32[2048,256]{1,0:T(8,128)} async-done(((f32[2048,2048]{1,0:T(8,128)}), f32[2048,256]{1,0:T(8,128)}) %reduce-scatter.17.cloned.1.call-update) | async-done | bytes 2097168 | tf_op jit(solution)/shard_map/reduce_scatter | solution.py:242
  886.3 120.4 %reduce-scatter.15.cloned.1.call-done = f32[256,2048]{1,0:T(8,128)} async-done(((f32[2048,2048]{1,0:T(8,128)}), f32[256,2048]{1,0:T(8,128)}) %reduce-scatter.15.cloned.1.call-update) | async-done | bytes 2097168 | tf_op jit(solution)/shard_map/reduce_scatter | solution.py:241
  (188 shorter events, 76.9 us)
Async XLA Ops:
  7.2 120.2 %all-gather.10.cloned.1.call-start = ((), (), s32[]{:S(2)}) async-start(), calls=%async_computation.8 | async-start | bytes 2359296 | tf_op jit(solution)/shard_map/all_gather | solution.py:146
  7.9 150.6 %all-gather.6.cloned.1.call-start = ((), (), s32[]{:S(2)}) async-start(), calls=%async_computation.6 | async-start | bytes 5242880 | tf_op jit(solution)/shard_map/all_gather | solution.py:155
  14.4 192.4 %all-gather.8.cloned.1.call-start = ((), (), s32[]{:S(2)}) async-start(), calls=%async_computation.7 | async-start | bytes 7077888 | tf_op jit(solution)/shard_map/all_gather | solution.py:145
  16.7 298.0 %all-gather.12.cloned.1.call-start = ((), (), s32[]{:S(2)}) async-start(), calls=%async_computation.9 | async-start | bytes 9437184 | tf_op jit(solution)/shard_map/all_gather | solution.py:147
  17.3 312.1 %all-gather.14.cloned.1.call-start = ((), (), s32[]{:S(2)}) async-start(), calls=%async_computation.10 | async-start | bytes 9437184 | tf_op jit(solution)/shard_map/all_gather | solution.py:148
  17.4 29.2 %collective-permute-start = (bf16[256,2048]{1,0:T(8,128)(2,1)S(1)}, bf16[256,2048]{1,0:T(8,128)(2,1)S(1)}, u32[]{:S(2)}, u32[]{:S(2)}) collective-permute-start(bf16[256,2048]{1,0:T(8,128)(2,1)S(1)} %copy-done.11), channel_id=1, source_target_pairs={{0,1},{1,2},{2,3},{3,0},{4,5},{5,6},{6,7},{7,4},{8,9},{9,10},{10,1... | collective-permute-start | bytes 3145736 | tf_op jit(solution)/shard_map/ppermute | solution.py:188
  20.5 87.4 %collective-permute-start.1 = (bf16[256,2048]{1,0:T(8,128)(2,1)S(1)}, bf16[256,2048]{1,0:T(8,128)(2,1)S(1)}, u32[]{:S(2)}, u32[]{:S(2)}) collective-permute-start(bf16[256,2048]{1,0:T(8,128)(2,1)S(1)} %copy-done.11), channel_id=1, source_target_pairs={{0,3},{1,0},{2,1},{3,2},{4,7},{5,4},{6,5},{7,6},{8,11},{9,8},{10,9... | collective-permute-start | bytes 3145736 | tf_op jit(solution)/shard_map/ppermute | solution.py:191
  22.6 452.4 %reduce-scatter.11.cloned.1.call-start = ((), (), s32[]{:S(2)}) async-start(), calls=%async_computation.13 | async-start | bytes 14155776 | tf_op jit(solution)/shard_map/reduce_scatter | solution.py:239
  46.5 79.8 %collective-permute-start.2 = (bf16[256,2048]{1,0:T(8,128)(2,1)S(1)}, bf16[256,2048]{1,0:T(8,128)(2,1)S(1)}, u32[]{:S(2)}, u32[]{:S(2)}) collective-permute-start(bf16[256,2048]{1,0:T(8,128)(2,1)S(1)} %collective-permute-done), channel_id=1, source_target_pairs={{0,1},{1,2},{2,3},{3,0},{4,5},{5,6},{6,7},{7,4},{8,9},{9,10},{10,1... | collective-permute-start | bytes 3145736 | tf_op jit(solution)/shard_map/ppermute | solution.py:188
  127.4 79.4 %copy-start.42 = (f32[3,512]{1,0:T(4,128)S(1)}, f32[3,512]{1,0:T(4,128)}, u32[]{:S(2)}) copy-start(f32[3,512]{1,0:T(4,128)} %param.26) | copy-start | bytes 18436
  224.6 20.9 %copy-start.23 = (f32[8,512]{1,0:T(8,128)}, f32[8,512]{1,0:T(8,128)S(1)}, u32[]{:S(2)}) copy-start(f32[8,512]{1,0:T(8,128)S(1)} %log_add_fusion.1) | copy-start | bytes 49156
  231.6 11.6 %copy-start.31 = (f32[8,512]{1,0:T(8,128)}, f32[8,512]{1,0:T(8,128)S(1)}, u32[]{:S(2)}) copy-start(f32[8,512]{1,0:T(8,128)S(1)} %fusion) | copy-start | bytes 49156
  245.5 19.0 %slice-start = ((s8[16777216]{0:T(1024)(128)(4,1)}), s8[4194304]{0:T(1024)(128)(4,1)S(1)}, s32[]{:S(2)}) async-start(s8[16777216]{0:T(1024)(128)(4,1)} %bitcast.132), calls=%async_computation.17 | async-start | bytes 8388608
  245.5 19.0 %slice-start.1 = ((s8[16777216]{0:T(1024)(128)(4,1)}), s8[4194304]{0:T(1024)(128)(4,1)S(1)}, s32[]{:S(2)}) async-start(s8[16777216]{0:T(1024)(128)(4,1)} %bitcast.132), calls=%async_computation.18 | async-start | bytes 8388608
  314.7 14.8 %copy-start.43 = (f32[2048]{0:T(1024)S(1)}, f32[2048]{0:T(1024)}, u32[]{:S(2)}) copy-start(f32[2048]{0:T(1024)} %param.30) | copy-start | bytes 24580
  314.7 248.1 %reduce-scatter.9.cloned.1.call-start = ((), (), s32[]{:S(2)}) async-start(), calls=%async_computation.12 | async-start | bytes 10485760 | tf_op jit(solution)/shard_map/reduce_scatter | solution.py:224
  329.4 23.0 %copy-start.41 = (bf16[2048,2048]{1,0:T(8,128)(2,1)S(1)}, bf16[2048,2048]{1,0:T(8,128)(2,1)}, u32[]{:S(2)}) copy-start(bf16[2048,2048]{1,0:T(8,128)(2,1)} %all-gather.12.cloned.1.call-done) | copy-start | bytes 25165828
  352.4 11.6 %copy-start.44 = (bf16[1024,2048]{1,0:T(8,128)(2,1)}, bf16[1024,2048]{1,0:T(8,128)(2,1)S(1)}, u32[]{:S(2)}) copy-start(bf16[1024,2048]{1,0:T(8,128)(2,1)S(1)} %get-tuple-element.98) | copy-start | bytes 12582916
  377.1 333.3 %reduce-scatter.7.cloned.1.call-start = ((), (), s32[]{:S(2)}) async-start(), calls=%async_computation.11 | async-start | bytes 10485760 | tf_op jit(solution)/shard_map/reduce_scatter | solution.py:178
  377.8 13.2 %slice-start.6 = ((s8[8388608]{0:T(1024)(128)(4,1)}), s8[4194304]{0:T(1024)(128)(4,1)S(1)}, s32[]{:S(2)}) async-start(s8[8388608]{0:T(1024)(128)(4,1)} %bitcast.158), calls=%async_computation.23 | async-start | bytes 8388608
  391.0 12.2 %copy-start.13 = (bf16[512,2048]{1,0:T(8,128)(2,1)S(1)}, bf16[512,2048]{1,0:T(8,128)(2,1)}, u32[]{:S(2)}) copy-start(bf16[512,2048]{1,0:T(8,128)(2,1)} %all-gather.10.cloned.1.call-done) | copy-start | bytes 6291460
  408.9 357.4 %reduce-scatter.13.cloned.1.call-start = ((), (), s32[]{:S(2)}) async-start(), calls=%async_computation.14 | async-start | bytes 4718592 | tf_op jit(solution)/shard_map/reduce_scatter | solution.py:240
  415.5 470.8 %reduce-scatter.17.cloned.1.call-start = ((), (), s32[]{:S(2)}) async-start(), calls=%async_computation.16 | async-start | bytes 18874368 | tf_op jit(solution)/shard_map/reduce_scatter | solution.py:242
  433.0 573.6 %reduce-scatter.15.cloned.1.call-start = ((), (), s32[]{:S(2)}) async-start(), calls=%async_computation.15 | async-start | bytes 18874368 | tf_op jit(solution)/shard_map/reduce_scatter | solution.py:241
  448.5 114.3 %copy-start.5 = (bf16[256,2048]{1,0:T(8,128)(2,1)S(1)}, bf16[256,2048]{1,0:T(8,128)(2,1)}, u32[]{:S(2)}) copy-start(bf16[256,2048]{1,0:T(8,128)(2,1)} %param.24) | copy-start | bytes 3145732
  448.5 114.3 %copy-start.24 = (f32[2048]{0:T(1024)S(1)}, f32[2048]{0:T(1024)}, u32[]{:S(2)}) copy-start(f32[2048]{0:T(1024)} %param.33) | copy-start | bytes 24580
  448.5 114.3 %copy-start.34 = (f32[256]{0:T(256)S(1)}, f32[256]{0:T(256)}, u32[]{:S(2)}) copy-start(f32[256]{0:T(256)} %copy-done.33) | copy-start | bytes 3076
  448.5 114.3 %copy-start.36 = (f32[256]{0:T(256)S(1)}, f32[256]{0:T(256)}, u32[]{:S(2)}) copy-start(f32[256]{0:T(256)} %copy-done.35) | copy-start | bytes 3076
  448.5 261.9 %copy-start.39 = (f32[2048]{0:T(1024)S(1)}, f32[2048]{0:T(1024)}, u32[]{:S(2)}) copy-start(f32[2048]{0:T(1024)} %param.32) | copy-start | bytes 24580
  448.5 261.9 %copy-start.40 = (f32[2048]{0:T(1024)S(1)}, f32[2048]{0:T(1024)}, u32[]{:S(2)}) copy-start(f32[2048]{0:T(1024)} %param.28) | copy-start | bytes 24580
  450.6 259.8 %copy-start.12 = (bf16[256,2048]{1,0:T(8,128)(2,1)S(1)}, bf16[256,2048]{1,0:T(8,128)(2,1)}, u32[]{:S(2)}) copy-start(bf16[256,2048]{1,0:T(8,128)(2,1)} %param.35) | copy-start | bytes 3145732
  756.8 250.4 %copy-start.38 = (f32[2048]{0:T(1024)}, f32[2048]{0:T(1024)S(1)}, u32[]{:S(2)}) copy-start(f32[2048]{0:T(1024)S(1)} %get-tuple-element.150) | copy-start | bytes 24580
  (35 other events, 188.9 us)
Sparse Core Ops, SparseCore 0:
  9.9 30.8 all-gather.9
  42.9 115.6 all-gather.5
  161.0 45.7 all-gather.7
  208.5 54.2 all-gather.11
  264.5 55.8 all-gather.13
  323.8 91.9 reduce-scatter.10
  418.1 144.6 reduce-scatter.8
  565.1 145.2 reduce-scatter.6
  714.4 51.8 reduce-scatter.12
  770.2 115.9 reduce-scatter.16
  890.4 116.1 reduce-scatter.14
